TPU v7x, 128 devices: a 2x2x16 block of a 8x8x16 slice. The times are simulated.
128 devices in a mesh: groups: 4 (over x, y), blk: 32 (over z, core).
Axes of the slice: x: 2, y: 2, z: 16, core: 2. Of those that a mesh axis runs over, the one named last changes fastest.
The devices are a block of a 8x8x16 slice.
Arguments:
- coords: float32 [32, 98304], P(None, ('groups', 'blk')), parts along dimension 1, may hold values from -6 to 6
- alpha: float32 [98304], P(('groups', 'blk')), parts along dimension 0, may hold values from -6 to 6
- probe_solves: float32 [15, 98304], P(None, ('groups', 'blk')), parts along dimension 1, may hold values from -6 to 6
- probes: float32 [15, 98304], P(None, ('groups', 'blk')), parts along dimension 1, may hold values from -6 to 6
- lengthscale: float32 [32], replicated, may hold values from 4 to 12
Outputs:
- grad: float32 [32, 98304], P(None, ('groups', 'blk')), parts along dimension 1
There are 4 independent parts, one for each index of `groups`. A program takes and returns all parts, laid end to end along the dimension named above; an argument that names none is the same for every part. Nothing has to cross between parts.
All inputs are finite; a program needn't handle non-finite values.
Results may differ from a plain program's by a relative error of at most 0.00014.
Values sent between devices are 32-bit elements; how exact they have to be, the bound alone decides.
A program may use at most 64 MiB of HBM per device.

v0:
```python
import jax
import jax.numpy as jnp
from jax import lax
from jax.sharding import PartitionSpec as P

root_five = 5.0**0.5


def shifted(value, axis, steps):
    count = lax.axis_size(axis)
    pairs = [(source, (source + steps) % count) for source in range(count)]
    return lax.ppermute(value, axis, pairs)


def tile_terms(own_scaled, own_table, vis_scaled, vis_table):
    probe_count = (own_table.shape[0] - 1) // 2
    half_inv = 1.0 / (2.0 * probe_count)
    left_rows = jnp.concatenate([own_table[:1], -half_inv * own_table[1:]], 0)
    right_rows = jnp.concatenate(
        [vis_table[:1], vis_table[1 + probe_count :], vis_table[1 : 1 + probe_count]], 0
    )
    contract_first = (((0,), (0,)), ((), ()))
    inner = lax.dot_general(
        own_scaled,
        vis_scaled,
        contract_first,
        precision=lax.Precision.HIGHEST,
        preferred_element_type=jnp.float32,
    )
    own_square = jnp.sum(own_scaled * own_scaled, 0)
    vis_square = jnp.sum(vis_scaled * vis_scaled, 0)
    distance = own_square[:, None] + vis_square[None, :] - 2.0 * inner
    radius = jnp.sqrt(jnp.maximum(distance, 0.0))
    profile = (1.0 + root_five * radius) * jnp.exp(-root_five * radius)
    coupling = lax.dot_general(
        left_rows,
        right_rows,
        contract_first,
        precision=lax.Precision.HIGHEST,
        preferred_element_type=jnp.float32,
    )
    weighted = coupling * profile
    row_part = own_scaled * jnp.sum(weighted, 1)[None, :] - lax.dot_general(
        vis_scaled,
        weighted,
        (((1,), (1,)), ((), ())),
        precision=lax.Precision.HIGHEST,
        preferred_element_type=jnp.float32,
    )
    col_part = vis_scaled * jnp.sum(weighted, 0)[None, :] - jnp.dot(
        own_scaled, weighted, precision=lax.Precision.HIGHEST, preferred_element_type=jnp.float32
    )
    return (row_part, col_part)


def on_device(coords, alpha, probe_solves, probes, lengthscale):
    scaled = coords / lengthscale[:, None]
    table = jnp.concatenate([alpha[None], probe_solves, probes], 0)
    step_count = lax.axis_size("blk") // 4
    vis_scaled, vis_table = shifted((scaled, table), "blk", -1)
    zero_field = jnp.zeros(scaled.shape, jnp.float32)

    def carry_step(index, state):
        cur_scaled, cur_table, col_acc, row_total = state
        row_part, col_part = tile_terms(scaled, table, cur_scaled, cur_table)
        moved = shifted((cur_scaled, cur_table, col_acc + col_part), "blk", -1)
        return (moved[0], moved[1], moved[2], row_total + row_part)

    cur_scaled, cur_table, col_acc, row_total = lax.fori_loop(
        0, step_count - 1, carry_step, (vis_scaled, vis_table, zero_field, zero_field)
    )
    row_part, col_part = tile_terms(scaled, table, cur_scaled, cur_table)
    row_total = row_total + row_part
    col_total = shifted(col_acc + col_part, "blk", step_count)
    return -(5.0 / 3.0) / lengthscale[:, None] * (row_total + col_total)


def solution(mesh):
    return jax.shard_map(
        on_device,
        mesh=mesh,
        in_specs=(
            P(None, ("groups", "blk")),
            P(("groups", "blk")),
            P(None, ("groups", "blk")),
            P(None, ("groups", "blk")),
            P(),
        ),
        out_specs=P(None, ("groups", "blk")),
        check_vma=False,
    )
```

profile of v0, /device:TPU:69, one launch (start us, length us, event | category | flops | bytes accessed | tf_op | source)
XLA Modules:
  0.0 128.9 jit_solution(11084534594902752604)
XLA Ops:
  1.0 9.9 %collective-permute-start.3 = (f32[32,768]{1,0:T(8,128)S(1)}, f32[32,768]{1,0:T(8,128)S(1)}, u32[]{:S(2)}, u32[]{:S(2)}) collective-permute-start(f32[32,768]{1,0:T(8,128)S(1)} %get-tuple-element.244), channel_id=1, source_target_pairs={{0,31},{1,0},{2,1},{3,2},{4,3},{5,4},{6,5},{7,6},{8,7},{9,8},{10,9... | collective-permute-start | bytes 294920 | tf_op jit(solution)/shard_map/ppermute | solution.py:12
  12.5 3.6 %collective-permute-start.4 = (f32[31,768]{1,0:T(8,128)S(1)}, f32[31,768]{1,0:T(8,128)S(1)}, u32[]{:S(2)}, u32[]{:S(2)}) collective-permute-start(f32[31,768]{1,0:T(8,128)S(1)} %fusion.14), channel_id=1, source_target_pairs={{0,31},{1,0},{2,1},{3,2},{4,3},{5,4},{6,5},{7,6},{8,7},{9,8},{10,9... | collective-permute-start | bytes 285704 | tf_op jit(solution)/shard_map/ppermute | solution.py:12
  17.6 92.7 %while.19 = (s32[]{:T(128)}, f32[32,768]{1,0:T(8,128)S(1)}, f32[31,768]{1,0:T(8,128)S(1)}, f32[32,768]{1,0:T(8,128)S(1)}, f32[32,768]{1,0:T(8,128)S(1)}, /*index...) while((s32[]{:T(128)}, f32[32,768]{1,0:T(8,128)S(1)}, ...), condition=%wide.region_5.0_spmd.clone, body=%wide.region_1.5_spmd.clone.sunk | while | flops 905693184 | bytes 15019247 | solution.py:69
  19.0 3.1 %collective-permute-start.1 = (f32[31,768]{1,0:T(8,128)S(1)}, f32[31,768]{1,0:T(8,128)S(1)}, u32[]{:S(2)}, u32[]{:S(2)}) collective-permute-start(f32[31,768]{1,0:T(8,128)S(1)} %copy.13), channel_id=1, source_target_pairs={{0,31},{1,0},{2,1},{3,2},{4,3},{5,4},{6,5},{7,6},{8,7},{9,8},{10,9... | collective-permute-start | bytes 285704 | tf_op jit(solution)/shard_map/while/body/eval_jaxpr/ppermute | solution.py:12
  22.1 2.1 %fusion.62 = f32[768,768]{1,0:T(8,128)S(1)} fusion(f32[30,768]{1,0:T(8,128)S(1)} %slice_multiply_fusion.2, f32[1,768]{1,0:T(1,128)S(1)} %get-tuple-element.264, f32[15,768]{1,0:T(8,128)S(1)} %get-tuple-element.231, f32[15,768]{1,0:T(8,128)S(1)} %get-tuple-element.232, f32[1,768]{1,0:T(1,128)S(1)} %slice.50), kind=kOutput, calls=%fused_computation.7.clone.1 | convolution fusion | flops 219485952 | bytes 2549760 | tf_op jit(solution)/shard_map/while/body/eval_jaxpr/dot_general | solution.py:35
  24.2 3.5 %fusion.63 = (f32[768]{0:T(1024)S(1)}, f32[768]{0:T(1024)S(1)}, f32[768,768]{1,0:T(8,128)S(1)}) fusion(f32[768,768]{1,0:T(8,128)S(1)} %fusion.62, f32[32,768]{1,0:T(8,128)S(1)} %get-tuple-element.266, f32[32,768]{1,0:T(8,128)S(1)} %copy.12, f32[768]{0:T(1024)S(1)} %multiply_reduce_fusion.4, f32[768]{0:T(1024)S(1)} %get-tuple-element.265), kind=kOutput, calls=%fused_computation.39.clone.1 | convolution fusion | flops 232978944 | bytes 4927488 | tf_op jit(solution)/shard_map/while/body/eval_jaxpr/dot_general | solution.py:23
  29.4 2.2 %fusion.65 = f32[32,768]{1,0:T(8,128)S(1)} fusion(f32[768,768]{1,0:T(8,128)S(1)} %get-tuple-element.233, f32[32,768]{1,0:T(8,128)S(1)} %copy.12, f32[32,768]{1,0:T(8,128)S(1)} %get-tuple-element.251, f32[32,768]{1,0:T(8,128)S(1)} %get-tuple-element.266, f32[768]{0:T(1024)S(1)} %get-tuple-element.235, pred[]{:T(512)S(6)} %compare.3), kind=kOutput, calls=%fused_computation.6.clone.1 | convolution fusion | flops 226590720 | bytes 2755585 | tf_op jit(solution)/shard_map/while/body/eval_jaxpr/dot_general | solution.py:43
  36.9 3.5 %fusion.63 = (f32[768]{0:T(1024)S(1)}, f32[768]{0:T(1024)S(1)}, f32[768,768]{1,0:T(8,128)S(1)}) fusion(f32[768,768]{1,0:T(8,128)S(1)} %fusion.62, f32[32,768]{1,0:T(8,128)S(1)} %get-tuple-element.266, f32[32,768]{1,0:T(8,128)S(1)} %copy.12, f32[768]{0:T(1024)S(1)} %multiply_reduce_fusion.4, f32[768]{0:T(1024)S(1)} %get-tuple-element.265), kind=kOutput, calls=%fused_computation.39.clone.1 | convolution fusion | flops 232978944 | bytes 4927488 | tf_op jit(solution)/shard_map/while/body/eval_jaxpr/dot_general | solution.py:23
  42.0 2.2 %fusion.65 = f32[32,768]{1,0:T(8,128)S(1)} fusion(f32[768,768]{1,0:T(8,128)S(1)} %get-tuple-element.233, f32[32,768]{1,0:T(8,128)S(1)} %copy.12, f32[32,768]{1,0:T(8,128)S(1)} %get-tuple-element.251, f32[32,768]{1,0:T(8,128)S(1)} %get-tuple-element.266, f32[768]{0:T(1024)S(1)} %get-tuple-element.235, pred[]{:T(512)S(6)} %compare.3), kind=kOutput, calls=%fused_computation.6.clone.1 | convolution fusion | flops 226590720 | bytes 2755585 | tf_op jit(solution)/shard_map/while/body/eval_jaxpr/dot_general | solution.py:43
  49.6 3.5 %fusion.63 = (f32[768]{0:T(1024)S(1)}, f32[768]{0:T(1024)S(1)}, f32[768,768]{1,0:T(8,128)S(1)}) fusion(f32[768,768]{1,0:T(8,128)S(1)} %fusion.62, f32[32,768]{1,0:T(8,128)S(1)} %get-tuple-element.266, f32[32,768]{1,0:T(8,128)S(1)} %copy.12, f32[768]{0:T(1024)S(1)} %multiply_reduce_fusion.4, f32[768]{0:T(1024)S(1)} %get-tuple-element.265), kind=kOutput, calls=%fused_computation.39.clone.1 | convolution fusion | flops 232978944 | bytes 4927488 | tf_op jit(solution)/shard_map/while/body/eval_jaxpr/dot_general | solution.py:23
  54.7 2.2 %fusion.65 = f32[32,768]{1,0:T(8,128)S(1)} fusion(f32[768,768]{1,0:T(8,128)S(1)} %get-tuple-element.233, f32[32,768]{1,0:T(8,128)S(1)} %copy.12, f32[32,768]{1,0:T(8,128)S(1)} %get-tuple-element.251, f32[32,768]{1,0:T(8,128)S(1)} %get-tuple-element.266, f32[768]{0:T(1024)S(1)} %get-tuple-element.235, pred[]{:T(512)S(6)} %compare.3), kind=kOutput, calls=%fused_computation.6.clone.1 | convolution fusion | flops 226590720 | bytes 2755585 | tf_op jit(solution)/shard_map/while/body/eval_jaxpr/dot_general | solution.py:43
  62.2 3.5 %fusion.63 = (f32[768]{0:T(1024)S(1)}, f32[768]{0:T(1024)S(1)}, f32[768,768]{1,0:T(8,128)S(1)}) fusion(f32[768,768]{1,0:T(8,128)S(1)} %fusion.62, f32[32,768]{1,0:T(8,128)S(1)} %get-tuple-element.266, f32[32,768]{1,0:T(8,128)S(1)} %copy.12, f32[768]{0:T(1024)S(1)} %multiply_reduce_fusion.4, f32[768]{0:T(1024)S(1)} %get-tuple-element.265), kind=kOutput, calls=%fused_computation.39.clone.1 | convolution fusion | flops 232978944 | bytes 4927488 | tf_op jit(solution)/shard_map/while/body/eval_jaxpr/dot_general | solution.py:23
  67.4 2.2 %fusion.65 = f32[32,768]{1,0:T(8,128)S(1)} fusion(f32[768,768]{1,0:T(8,128)S(1)} %get-tuple-element.233, f32[32,768]{1,0:T(8,128)S(1)} %copy.12, f32[32,768]{1,0:T(8,128)S(1)} %get-tuple-element.251, f32[32,768]{1,0:T(8,128)S(1)} %get-tuple-element.266, f32[768]{0:T(1024)S(1)} %get-tuple-element.235, pred[]{:T(512)S(6)} %compare.3), kind=kOutput, calls=%fused_computation.6.clone.1 | convolution fusion | flops 226590720 | bytes 2755585 | tf_op jit(solution)/shard_map/while/body/eval_jaxpr/dot_general | solution.py:43
  71.5 2.2 %collective-permute-start.1 = (f32[31,768]{1,0:T(8,128)S(1)}, f32[31,768]{1,0:T(8,128)S(1)}, u32[]{:S(2)}, u32[]{:S(2)}) collective-permute-start(f32[31,768]{1,0:T(8,128)S(1)} %copy.13), channel_id=1, source_target_pairs={{0,31},{1,0},{2,1},{3,2},{4,3},{5,4},{6,5},{7,6},{8,7},{9,8},{10,9... | collective-permute-start | bytes 285704 | tf_op jit(solution)/shard_map/while/body/eval_jaxpr/ppermute | solution.py:12
  75.9 3.5 %fusion.63 = (f32[768]{0:T(1024)S(1)}, f32[768]{0:T(1024)S(1)}, f32[768,768]{1,0:T(8,128)S(1)}) fusion(f32[768,768]{1,0:T(8,128)S(1)} %fusion.62, f32[32,768]{1,0:T(8,128)S(1)} %get-tuple-element.266, f32[32,768]{1,0:T(8,128)S(1)} %copy.12, f32[768]{0:T(1024)S(1)} %multiply_reduce_fusion.4, f32[768]{0:T(1024)S(1)} %get-tuple-element.265), kind=kOutput, calls=%fused_computation.39.clone.1 | convolution fusion | flops 232978944 | bytes 4927488 | tf_op jit(solution)/shard_map/while/body/eval_jaxpr/dot_general | solution.py:23
  81.0 2.2 %fusion.65 = f32[32,768]{1,0:T(8,128)S(1)} fusion(f32[768,768]{1,0:T(8,128)S(1)} %get-tuple-element.233, f32[32,768]{1,0:T(8,128)S(1)} %copy.12, f32[32,768]{1,0:T(8,128)S(1)} %get-tuple-element.251, f32[32,768]{1,0:T(8,128)S(1)} %get-tuple-element.266, f32[768]{0:T(1024)S(1)} %get-tuple-element.235, pred[]{:T(512)S(6)} %compare.3), kind=kOutput, calls=%fused_computation.6.clone.1 | convolution fusion | flops 226590720 | bytes 2755585 | tf_op jit(solution)/shard_map/while/body/eval_jaxpr/dot_general | solution.py:43
  88.6 3.5 %fusion.63 = (f32[768]{0:T(1024)S(1)}, f32[768]{0:T(1024)S(1)}, f32[768,768]{1,0:T(8,128)S(1)}) fusion(f32[768,768]{1,0:T(8,128)S(1)} %fusion.62, f32[32,768]{1,0:T(8,128)S(1)} %get-tuple-element.266, f32[32,768]{1,0:T(8,128)S(1)} %copy.12, f32[768]{0:T(1024)S(1)} %multiply_reduce_fusion.4, f32[768]{0:T(1024)S(1)} %get-tuple-element.265), kind=kOutput, calls=%fused_computation.39.clone.1 | convolution fusion | flops 232978944 | bytes 4927488 | tf_op jit(solution)/shard_map/while/body/eval_jaxpr/dot_general | solution.py:23
  93.7 2.2 %fusion.65 = f32[32,768]{1,0:T(8,128)S(1)} fusion(f32[768,768]{1,0:T(8,128)S(1)} %get-tuple-element.233, f32[32,768]{1,0:T(8,128)S(1)} %copy.12, f32[32,768]{1,0:T(8,128)S(1)} %get-tuple-element.251, f32[32,768]{1,0:T(8,128)S(1)} %get-tuple-element.266, f32[768]{0:T(1024)S(1)} %get-tuple-element.235, pred[]{:T(512)S(6)} %compare.3), kind=kOutput, calls=%fused_computation.6.clone.1 | convolution fusion | flops 226590720 | bytes 2755585 | tf_op jit(solution)/shard_map/while/body/eval_jaxpr/dot_general | solution.py:43
  101.2 3.5 %fusion.63 = (f32[768]{0:T(1024)S(1)}, f32[768]{0:T(1024)S(1)}, f32[768,768]{1,0:T(8,128)S(1)}) fusion(f32[768,768]{1,0:T(8,128)S(1)} %fusion.62, f32[32,768]{1,0:T(8,128)S(1)} %get-tuple-element.266, f32[32,768]{1,0:T(8,128)S(1)} %copy.12, f32[768]{0:T(1024)S(1)} %multiply_reduce_fusion.4, f32[768]{0:T(1024)S(1)} %get-tuple-element.265), kind=kOutput, calls=%fused_computation.39.clone.1 | convolution fusion | flops 232978944 | bytes 4927488 | tf_op jit(solution)/shard_map/while/body/eval_jaxpr/dot_general | solution.py:23
  106.4 2.2 %fusion.65 = f32[32,768]{1,0:T(8,128)S(1)} fusion(f32[768,768]{1,0:T(8,128)S(1)} %get-tuple-element.233, f32[32,768]{1,0:T(8,128)S(1)} %copy.12, f32[32,768]{1,0:T(8,128)S(1)} %get-tuple-element.251, f32[32,768]{1,0:T(8,128)S(1)} %get-tuple-element.266, f32[768]{0:T(1024)S(1)} %get-tuple-element.235, pred[]{:T(512)S(6)} %compare.3), kind=kOutput, calls=%fused_computation.6.clone.1 | convolution fusion | flops 226590720 | bytes 2755585 | tf_op jit(solution)/shard_map/while/body/eval_jaxpr/dot_general | solution.py:43
  112.5 3.5 %fusion.24 = (f32[768]{0:T(1024)S(1)}, f32[768]{0:T(1024)S(1)}, f32[768,768]{1,0:T(8,128)S(1)}) fusion(f32[768,768]{1,0:T(8,128)S(1)} %fusion.15, f32[32,768]{1,0:T(8,128)S(1)} %get-tuple-element.271, f32[32,768]{1,0:T(8,128)S(1)} %get-tuple-element.109, f32[768]{0:T(1024)S(1)} %multiply_reduce_fusion.1, f32[768]{0:T(1024)S(1)} %get-tuple-element.283), kind=kOutput, calls=%fused_computation.40 | convolution fusion | flops 232978944 | bytes 4927488 | tf_op jit(solution)/shard_map/dot_general | solution.py:23
  117.5 3.0 %collective-permute-start.5 = (f32[32,768]{1,0:T(8,128)S(1)}, f32[32,768]{1,0:T(8,128)S(1)}, u32[]{:S(2)}, u32[]{:S(2)}) collective-permute-start(f32[32,768]{1,0:T(8,128)S(1)} %subtract_add_fusion), channel_id=1, source_target_pairs={{0,8},{1,9},{2,10},{3,11},{4,12},{5,13},{6,14},{7,15},{8,16},{9,17... | collective-permute-start | bytes 294920 | tf_op jit(solution)/shard_map/ppermute | solution.py:12
  120.5 2.2 %convolution_subtract_fusion = f32[32,768]{1,0:T(8,128)S(1)} fusion(f32[32,768]{1,0:T(8,128)S(1)} %get-tuple-element.109, f32[768,768]{1,0:T(8,128)S(1)} %get-tuple-element.170, f32[32,768]{1,0:T(8,128)S(1)} %get-tuple-element.271, f32[768]{0:T(1024)S(1)} %get-tuple-element.143), kind=kOutput, calls=%fused_computation.20 | convolution fusion | flops 226541568 | bytes 2657280 | tf_op jit(solution)/shard_map/dot_general | solution.py:43
  122.7 5.4 %collective-permute-done.5 = f32[32,768]{1,0:T(8,128)S(1)} collective-permute-done((f32[32,768]{1,0:T(8,128)S(1)}, f32[32,768]{1,0:T(8,128)S(1)}, u32[]{:S(2)}, u32[]{:S(2)}) %collective-permute-start.5) | collective-permute-done | bytes 98336 | tf_op jit(solution)/shard_map/ppermute | solution.py:12
  (111 shorter events, 53.0 us)
Async XLA Ops:
  1.0 16.6 %collective-permute-start.3 = (f32[32,768]{1,0:T(8,128)S(1)}, f32[32,768]{1,0:T(8,128)S(1)}, u32[]{:S(2)}, u32[]{:S(2)}) collective-permute-start(f32[32,768]{1,0:T(8,128)S(1)} %get-tuple-element.244), channel_id=1, source_target_pairs={{0,31},{1,0},{2,1},{3,2},{4,3},{5,4},{6,5},{7,6},{8,7},{9,8},{10,9... | collective-permute-start | bytes 294920 | tf_op jit(solution)/shard_map/ppermute | solution.py:12
  12.5 5.1 %collective-permute-start.4 = (f32[31,768]{1,0:T(8,128)S(1)}, f32[31,768]{1,0:T(8,128)S(1)}, u32[]{:S(2)}, u32[]{:S(2)}) collective-permute-start(f32[31,768]{1,0:T(8,128)S(1)} %fusion.14), channel_id=1, source_target_pairs={{0,31},{1,0},{2,1},{3,2},{4,3},{5,4},{6,5},{7,6},{8,7},{9,8},{10,9... | collective-permute-start | bytes 285704 | tf_op jit(solution)/shard_map/ppermute | solution.py:12
  17.6 15.7 %collective-permute-start = (f32[32,768]{1,0:T(8,128)S(1)}, f32[32,768]{1,0:T(8,128)S(1)}, u32[]{:S(2)}, u32[]{:S(2)}) collective-permute-start(f32[32,768]{1,0:T(8,128)S(1)} %copy.12), channel_id=1, source_target_pairs={{0,31},{1,0},{2,1},{3,2},{4,3},{5,4},{6,5},{7,6},{8,7},{9,8},{10,9... | collective-permute-start | bytes 294920 | tf_op jit(solution)/shard_map/while/body/eval_jaxpr/ppermute | solution.py:12
  19.0 12.6 %collective-permute-start.1 = (f32[31,768]{1,0:T(8,128)S(1)}, f32[31,768]{1,0:T(8,128)S(1)}, u32[]{:S(2)}, u32[]{:S(2)}) collective-permute-start(f32[31,768]{1,0:T(8,128)S(1)} %copy.13), channel_id=1, source_target_pairs={{0,31},{1,0},{2,1},{3,2},{4,3},{5,4},{6,5},{7,6},{8,7},{9,8},{10,9... | collective-permute-start | bytes 285704 | tf_op jit(solution)/shard_map/while/body/eval_jaxpr/ppermute | solution.py:12
  29.3 4.1 %collective-permute-start.2 = (f32[32,768]{1,0:T(8,128)S(1)}, f32[32,768]{1,0:T(8,128)S(1)}, u32[]{:S(2)}, u32[]{:S(2)}) collective-permute-start(f32[32,768]{1,0:T(8,128)S(1)} %fusion.64), channel_id=1, source_target_pairs={{0,31},{1,0},{2,1},{3,2},{4,3},{5,4},{6,5},{7,6},{8,7},{9,8},{10,9... | collective-permute-start | bytes 294920 | tf_op jit(solution)/shard_map/while/body/eval_jaxpr/ppermute | solution.py:12
  33.4 12.7 %collective-permute-start = (f32[32,768]{1,0:T(8,128)S(1)}, f32[32,768]{1,0:T(8,128)S(1)}, u32[]{:S(2)}, u32[]{:S(2)}) collective-permute-start(f32[32,768]{1,0:T(8,128)S(1)} %copy.12), channel_id=1, source_target_pairs={{0,31},{1,0},{2,1},{3,2},{4,3},{5,4},{6,5},{7,6},{8,7},{9,8},{10,9... | collective-permute-start | bytes 294920 | tf_op jit(solution)/shard_map/while/body/eval_jaxpr/ppermute | solution.py:12
  33.5 10.8 %collective-permute-start.1 = (f32[31,768]{1,0:T(8,128)S(1)}, f32[31,768]{1,0:T(8,128)S(1)}, u32[]{:S(2)}, u32[]{:S(2)}) collective-permute-start(f32[31,768]{1,0:T(8,128)S(1)} %copy.13), channel_id=1, source_target_pairs={{0,31},{1,0},{2,1},{3,2},{4,3},{5,4},{6,5},{7,6},{8,7},{9,8},{10,9... | collective-permute-start | bytes 285704 | tf_op jit(solution)/shard_map/while/body/eval_jaxpr/ppermute | solution.py:12
  41.9 4.1 %collective-permute-start.2 = (f32[32,768]{1,0:T(8,128)S(1)}, f32[32,768]{1,0:T(8,128)S(1)}, u32[]{:S(2)}, u32[]{:S(2)}) collective-permute-start(f32[32,768]{1,0:T(8,128)S(1)} %fusion.64), channel_id=1, source_target_pairs={{0,31},{1,0},{2,1},{3,2},{4,3},{5,4},{6,5},{7,6},{8,7},{9,8},{10,9... | collective-permute-start | bytes 294920 | tf_op jit(solution)/shard_map/while/body/eval_jaxpr/ppermute | solution.py:12
  46.0 12.7 %collective-permute-start = (f32[32,768]{1,0:T(8,128)S(1)}, f32[32,768]{1,0:T(8,128)S(1)}, u32[]{:S(2)}, u32[]{:S(2)}) collective-permute-start(f32[32,768]{1,0:T(8,128)S(1)} %copy.12), channel_id=1, source_target_pairs={{0,31},{1,0},{2,1},{3,2},{4,3},{5,4},{6,5},{7,6},{8,7},{9,8},{10,9... | collective-permute-start | bytes 294920 | tf_op jit(solution)/shard_map/while/body/eval_jaxpr/ppermute | solution.py:12
  46.1 10.8 %collective-permute-start.1 = (f32[31,768]{1,0:T(8,128)S(1)}, f32[31,768]{1,0:T(8,128)S(1)}, u32[]{:S(2)}, u32[]{:S(2)}) collective-permute-start(f32[31,768]{1,0:T(8,128)S(1)} %copy.13), channel_id=1, source_target_pairs={{0,31},{1,0},{2,1},{3,2},{4,3},{5,4},{6,5},{7,6},{8,7},{9,8},{10,9... | collective-permute-start | bytes 285704 | tf_op jit(solution)/shard_map/while/body/eval_jaxpr/ppermute | solution.py:12
  54.6 4.1 %collective-permute-start.2 = (f32[32,768]{1,0:T(8,128)S(1)}, f32[32,768]{1,0:T(8,128)S(1)}, u32[]{:S(2)}, u32[]{:S(2)}) collective-permute-start(f32[32,768]{1,0:T(8,128)S(1)} %fusion.64), channel_id=1, source_target_pairs={{0,31},{1,0},{2,1},{3,2},{4,3},{5,4},{6,5},{7,6},{8,7},{9,8},{10,9... | collective-permute-start | bytes 294920 | tf_op jit(solution)/shard_map/while/body/eval_jaxpr/ppermute | solution.py:12
  58.7 12.7 %collective-permute-start = (f32[32,768]{1,0:T(8,128)S(1)}, f32[32,768]{1,0:T(8,128)S(1)}, u32[]{:S(2)}, u32[]{:S(2)}) collective-permute-start(f32[32,768]{1,0:T(8,128)S(1)} %copy.12), channel_id=1, source_target_pairs={{0,31},{1,0},{2,1},{3,2},{4,3},{5,4},{6,5},{7,6},{8,7},{9,8},{10,9... | collective-permute-start | bytes 294920 | tf_op jit(solution)/shard_map/while/body/eval_jaxpr/ppermute | solution.py:12
  58.8 10.8 %collective-permute-start.1 = (f32[31,768]{1,0:T(8,128)S(1)}, f32[31,768]{1,0:T(8,128)S(1)}, u32[]{:S(2)}, u32[]{:S(2)}) collective-permute-start(f32[31,768]{1,0:T(8,128)S(1)} %copy.13), channel_id=1, source_target_pairs={{0,31},{1,0},{2,1},{3,2},{4,3},{5,4},{6,5},{7,6},{8,7},{9,8},{10,9... | collective-permute-start | bytes 285704 | tf_op jit(solution)/shard_map/while/body/eval_jaxpr/ppermute | solution.py:12
  67.3 4.1 %collective-permute-start.2 = (f32[32,768]{1,0:T(8,128)S(1)}, f32[32,768]{1,0:T(8,128)S(1)}, u32[]{:S(2)}, u32[]{:S(2)}) collective-permute-start(f32[32,768]{1,0:T(8,128)S(1)} %fusion.64), channel_id=1, source_target_pairs={{0,31},{1,0},{2,1},{3,2},{4,3},{5,4},{6,5},{7,6},{8,7},{9,8},{10,9... | collective-permute-start | bytes 294920 | tf_op jit(solution)/shard_map/while/body/eval_jaxpr/ppermute | solution.py:12
  71.4 13.6 %collective-permute-start = (f32[32,768]{1,0:T(8,128)S(1)}, f32[32,768]{1,0:T(8,128)S(1)}, u32[]{:S(2)}, u32[]{:S(2)}) collective-permute-start(f32[32,768]{1,0:T(8,128)S(1)} %copy.12), channel_id=1, source_target_pairs={{0,31},{1,0},{2,1},{3,2},{4,3},{5,4},{6,5},{7,6},{8,7},{9,8},{10,9... | collective-permute-start | bytes 294920 | tf_op jit(solution)/shard_map/while/body/eval_jaxpr/ppermute | solution.py:12
  71.5 11.8 %collective-permute-start.1 = (f32[31,768]{1,0:T(8,128)S(1)}, f32[31,768]{1,0:T(8,128)S(1)}, u32[]{:S(2)}, u32[]{:S(2)}) collective-permute-start(f32[31,768]{1,0:T(8,128)S(1)} %copy.13), channel_id=1, source_target_pairs={{0,31},{1,0},{2,1},{3,2},{4,3},{5,4},{6,5},{7,6},{8,7},{9,8},{10,9... | collective-permute-start | bytes 285704 | tf_op jit(solution)/shard_map/while/body/eval_jaxpr/ppermute | solution.py:12
  80.9 4.1 %collective-permute-start.2 = (f32[32,768]{1,0:T(8,128)S(1)}, f32[32,768]{1,0:T(8,128)S(1)}, u32[]{:S(2)}, u32[]{:S(2)}) collective-permute-start(f32[32,768]{1,0:T(8,128)S(1)} %fusion.64), channel_id=1, source_target_pairs={{0,31},{1,0},{2,1},{3,2},{4,3},{5,4},{6,5},{7,6},{8,7},{9,8},{10,9... | collective-permute-start | bytes 294920 | tf_op jit(solution)/shard_map/while/body/eval_jaxpr/ppermute | solution.py:12
  85.0 12.7 %collective-permute-start = (f32[32,768]{1,0:T(8,128)S(1)}, f32[32,768]{1,0:T(8,128)S(1)}, u32[]{:S(2)}, u32[]{:S(2)}) collective-permute-start(f32[32,768]{1,0:T(8,128)S(1)} %copy.12), channel_id=1, source_target_pairs={{0,31},{1,0},{2,1},{3,2},{4,3},{5,4},{6,5},{7,6},{8,7},{9,8},{10,9... | collective-permute-start | bytes 294920 | tf_op jit(solution)/shard_map/while/body/eval_jaxpr/ppermute | solution.py:12
  85.1 10.8 %collective-permute-start.1 = (f32[31,768]{1,0:T(8,128)S(1)}, f32[31,768]{1,0:T(8,128)S(1)}, u32[]{:S(2)}, u32[]{:S(2)}) collective-permute-start(f32[31,768]{1,0:T(8,128)S(1)} %copy.13), channel_id=1, source_target_pairs={{0,31},{1,0},{2,1},{3,2},{4,3},{5,4},{6,5},{7,6},{8,7},{9,8},{10,9... | collective-permute-start | bytes 285704 | tf_op jit(solution)/shard_map/while/body/eval_jaxpr/ppermute | solution.py:12
  93.6 4.1 %collective-permute-start.2 = (f32[32,768]{1,0:T(8,128)S(1)}, f32[32,768]{1,0:T(8,128)S(1)}, u32[]{:S(2)}, u32[]{:S(2)}) collective-permute-start(f32[32,768]{1,0:T(8,128)S(1)} %fusion.64), channel_id=1, source_target_pairs={{0,31},{1,0},{2,1},{3,2},{4,3},{5,4},{6,5},{7,6},{8,7},{9,8},{10,9... | collective-permute-start | bytes 294920 | tf_op jit(solution)/shard_map/while/body/eval_jaxpr/ppermute | solution.py:12
  97.7 12.7 %collective-permute-start = (f32[32,768]{1,0:T(8,128)S(1)}, f32[32,768]{1,0:T(8,128)S(1)}, u32[]{:S(2)}, u32[]{:S(2)}) collective-permute-start(f32[32,768]{1,0:T(8,128)S(1)} %copy.12), channel_id=1, source_target_pairs={{0,31},{1,0},{2,1},{3,2},{4,3},{5,4},{6,5},{7,6},{8,7},{9,8},{10,9... | collective-permute-start | bytes 294920 | tf_op jit(solution)/shard_map/while/body/eval_jaxpr/ppermute | solution.py:12
  97.8 10.8 %collective-permute-start.1 = (f32[31,768]{1,0:T(8,128)S(1)}, f32[31,768]{1,0:T(8,128)S(1)}, u32[]{:S(2)}, u32[]{:S(2)}) collective-permute-start(f32[31,768]{1,0:T(8,128)S(1)} %copy.13), channel_id=1, source_target_pairs={{0,31},{1,0},{2,1},{3,2},{4,3},{5,4},{6,5},{7,6},{8,7},{9,8},{10,9... | collective-permute-start | bytes 285704 | tf_op jit(solution)/shard_map/while/body/eval_jaxpr/ppermute | solution.py:12
  106.3 4.1 %collective-permute-start.2 = (f32[32,768]{1,0:T(8,128)S(1)}, f32[32,768]{1,0:T(8,128)S(1)}, u32[]{:S(2)}, u32[]{:S(2)}) collective-permute-start(f32[32,768]{1,0:T(8,128)S(1)} %fusion.64), channel_id=1, source_target_pairs={{0,31},{1,0},{2,1},{3,2},{4,3},{5,4},{6,5},{7,6},{8,7},{9,8},{10,9... | collective-permute-start | bytes 294920 | tf_op jit(solution)/shard_map/while/body/eval_jaxpr/ppermute | solution.py:12
  117.5 10.7 %collective-permute-start.5 = (f32[32,768]{1,0:T(8,128)S(1)}, f32[32,768]{1,0:T(8,128)S(1)}, u32[]{:S(2)}, u32[]{:S(2)}) collective-permute-start(f32[32,768]{1,0:T(8,128)S(1)} %subtract_add_fusion), channel_id=1, source_target_pairs={{0,8},{1,9},{2,10},{3,11},{4,12},{5,13},{6,14},{7,15},{8,16},{9,17... | collective-permute-start | bytes 294920 | tf_op jit(solution)/shard_map/ppermute | solution.py:12
where the time goes:
time: 130 us; the launch traced here: 129 us
  matrix products  74.4 us (57%)
  starting transfers between devices  30.7 us (24%)
  waiting for transfers between devices  17.8 us (14%)
  other arithmetic  4.33 us (3%)
    ppermute x24, starting transfers between devices, shifted(): return lax.ppermute(value, axis, pairs)  30.7 us
    dot_general x8, matrix products, tile_terms(): lax.dot_general(own_scaled, vis_scaled, contract_first, precision=lax.Pre...  28.1 us
    ppermute x24, waiting for transfers between devices, shifted(): return lax.ppermute(value, axis, pairs)  17.8 us
    dot_general x8, matrix products, tile_terms(): lax.dot_general(vis_scaled, weighted, (((1,), (1,)), ((), ())), precision...  17.7 us
    dot_general x8, matrix products, tile_terms(): lax.dot_general(left_rows, right_rows, contract_first, precision=lax.Prec...  16.4 us
    dot_general x8, matrix products, tile_terms(): jnp.dot(own_scaled, weighted, precision=lax.Precision.HIGHEST, preferred_...  12.2 us
  transfers between devices with their start and end apart: 24, of which 8 were waited for; matrix products, arithmetic and copies ran while one was open for 55% of the time, Pallas kernels for 0%

commit v1 on v0

v1 whole, which is shorter than its diff:
```python
import functools
import math

import jax
import jax.numpy as jnp
from jax import lax
from jax.experimental import pallas as pl
from jax.experimental.pallas import tpu as pltpu
from jax.sharding import PartitionSpec as P

F32 = jnp.float32
BF16 = jnp.bfloat16
MESH = pl.DeviceIdType.MESH

UNIT = math.sqrt(5.0) * math.log2(math.e)
LN2 = math.log(2.0)

CHUNK = 256
DEPTH = 208
OWN, PARTNER, UP, DOWN, P_UP, P_DOWN, SLOTS = 0, 1, 2, 6, 10, 14, 18


def split3(x):
    hi = x.astype(BF16)
    rest = x - hi.astype(F32)
    mid = rest.astype(BF16)
    lo = (rest - mid.astype(F32)).astype(BF16)
    return hi, mid, lo


def split2(x):
    hi = x.astype(BF16)
    return hi, (x - hi.astype(F32)).astype(BF16)


def column_of(row, dim):
    sub = lax.broadcasted_iota(jnp.int32, (dim, dim), 0)
    lane = lax.broadcasted_iota(jnp.int32, (dim, dim), 1)
    full = jnp.broadcast_to(row, (dim, dim))
    return jnp.sum(jnp.where(sub == lane, full, 0.0), axis=1, keepdims=True)


def pick_rows(rows, shape):
    sub = lax.broadcasted_iota(jnp.int32, shape, 0)
    out = jnp.zeros(shape, F32)
    for index, value in enumerate(rows):
        out = jnp.where(sub == index, value, out)
    return out


def prepare(block, scale_ref, rhs_d, rhs_c, vis):
    scaled = block[0:32, :] * scale_ref[...]
    hi, mid, lo = split3(scaled)
    for index, value in enumerate((hi, mid, lo, hi, mid, hi)):
        rhs_d[32 * index : 32 * index + 32, :] = value
    n_hi, n_mid, n_lo = split3(jnp.sum(scaled * scaled, 0, keepdims=True))
    ends = (1.0, 1.0, 1.0, n_hi.astype(F32), n_mid.astype(F32), n_lo.astype(F32))
    rhs_d[192:208, :] = pick_rows(ends, (16, CHUNK)).astype(BF16)
    t_hi, t_lo = split2(block[32:64, :])
    for index, value in enumerate((t_hi, t_lo, t_hi, t_lo)):
        rhs_c[32 * index : 32 * index + 32, :] = value
    for side in (0, CHUNK):
        vis[0:32, side : side + CHUNK] = hi
        vis[32:64, side : side + CHUNK] = mid


def products(lhs_d, lhs_c, rhs_d, rhs_c, dist, coup):
    dist[...] = jnp.dot(lhs_d[:, 0:DEPTH], rhs_d[...], preferred_element_type=F32)
    coup[...] = jnp.dot(lhs_c[...], rhs_c[...], preferred_element_type=F32)


def weigh(dist, coup, w, rows=128):
    for start in range(0, dist.shape[0], rows):
        part = pl.ds(start, rows)
        d2 = jnp.maximum(dist[part, :], 1e-30)
        u = d2 * lax.rsqrt(d2)
        weight = (1.0 / LN2 + u) * jnp.exp2(-u) * coup[part, :]
        hi, lo = split2(weight)
        w[part, 0:CHUNK] = hi
        w[part, CHUNK : 2 * CHUNK] = lo


def gather_sums(vis, w, total):
    total[...] += lax.dot_general(
        vis[...], w[...], (((1,), (1,)), ((), ())), preferred_element_type=F32
    )


def own_side(buf, scale_ref, lhs_d, lhs_c, chunks, probe_count):
    sub = lax.broadcasted_iota(jnp.int32, (32, CHUNK), 0)
    for q in range(chunks):
        block = buf[OWN, q]
        scaled = block[0:32, :] * scale_ref[...]
        hi, mid, lo = (-2.0 * v.astype(F32) for v in split3(scaled))
        norm = [v.astype(F32) for v in split3(jnp.sum(scaled * scaled, 0, keepdims=True))]
        ends = pick_rows((*norm, 1.0, 1.0, 1.0), (64, CHUNK))
        stack = jnp.concatenate([hi, hi, hi, mid, mid, lo, ends], 0)
        lhs_d[q * CHUNK : (q + 1) * CHUNK, :] = stack.T.astype(BF16)
        swapped = jnp.concatenate([block[48:64, :], block[32:48, :]], 0)
        half_inv = LN2 / (2.0 * probe_count)
        table = jnp.where(
            sub == probe_count,
            LN2 * swapped,
            jnp.where(sub == 2 * probe_count + 1, 0.0, -half_inv * swapped),
        )
        t_hi, t_lo = (v.astype(F32) for v in split2(table))
        stack = jnp.concatenate([t_hi, t_hi, t_lo, t_lo], 0)
        lhs_c[q * CHUNK : (q + 1) * CHUNK, :] = stack.T.astype(BF16)


def kernel(size, coords, alpha, solves, probes, length, out, *scratch):
    (buf, scale_ref, lhs_d, lhs_c, rhs_d0, rhs_d1, rhs_c0, rhs_c1, v0, v1, v2, v3,
     dist0, dist1, coup0, coup1, w0, w1, total, send_sem, recv_sem) = scratch
    rhs_d, rhs_c, vis = (rhs_d0, rhs_d1), (rhs_c0, rhs_c1), (v0, v1, v2, v3)
    dist, coup, w = (dist0, dist1), (coup0, coup1), (w0, w1)
    dim, points = coords.shape
    probe_count = solves.shape[0]
    chunks = points // CHUNK
    hops = size // 8
    passes = hops * chunks

    group = lax.axis_index("groups")
    me = lax.axis_index("blk")
    core = lax.rem(me, 2)
    above = lax.rem(me + 2, size)
    below = lax.rem(me + size - 2, size)
    partner = me + 1 - 2 * core

    for q in range(chunks):
        lanes = slice(q * CHUNK, (q + 1) * CHUNK)
        buf[OWN, q, 0:32, :] = coords[:, lanes]
        buf[OWN, q, 32:64, :] = jnp.concatenate(
            [solves[:, lanes], alpha[:, lanes], probes[:, lanes], alpha[:, lanes]], 0
        )

    barrier = pltpu.get_barrier_semaphore()
    for other in (above, below, partner):
        pl.semaphore_signal(barrier, inc=1, device_id=(group, other), device_id_type=MESH)
    pl.semaphore_wait(barrier, 3)

    def send(src, dst, q, other):
        return pltpu.make_async_remote_copy(
            src_ref=buf.at[src, q],
            dst_ref=buf.at[dst, q],
            send_sem=send_sem.at[dst, q],
            recv_sem=recv_sem.at[dst, q],
            device_id=(group, other),
            device_id_type=MESH,
        )

    def arrived(slot, q):
        send(slot, slot, q, partner).wait_recv()

    for q in range(chunks):
        send(OWN, UP, q, above).start()
        send(OWN, DOWN, q, below).start()
        send(OWN, PARTNER, q, partner).start()

    give_src = jnp.where(core == 0, DOWN + hops - 1, UP + hops - 1)
    give_dst = jnp.where(core == 0, P_DOWN + hops - 1, P_UP + hops - 1)
    take = jnp.where(core == 0, P_UP + hops - 1, P_DOWN + hops - 1)

    def relay(k):
        hop, q = k // chunks, lax.rem(k, chunks)
        arrived(UP + hop, q)

        @pl.when(hop < hops - 1)
        def _():
            send(UP + hop, UP + hop + 1, q, above).start()

        arrived(DOWN + hop, q)

        @pl.when(hop < hops - 1)
        def _():
            send(DOWN + hop, DOWN + hop + 1, q, below).start()
            send(UP + hop, P_UP + hop, q, partner).start()
            send(DOWN + hop, P_DOWN + hop, q, partner).start()

        @pl.when(hop == hops - 1)
        def _():
            send(give_src, give_dst, q, partner).start()

    def extra(e):
        pair = jnp.maximum(e - chunks, 0)
        k = pair // 2
        lane = jnp.where(lax.rem(pair, 2) == 0, P_UP, P_DOWN)
        tail = e - chunks - 2 * (passes - chunks)
        slot = jnp.where(
            e < chunks,
            PARTNER,
            jnp.where(tail < 0, lane + k // chunks, take),
        )
        q = jnp.where(e < chunks, e, jnp.where(tail < 0, lax.rem(k, chunks), tail))
        return slot, q

    def place(k, position):
        e_slot, e_q = extra(2 * k + (1 if position else 0))
        hop, q = k // chunks, lax.rem(k, chunks)
        if position == 0:
            return e_slot, e_q
        last = k == passes - 1
        order = {1: (e_slot, UP + hop), 2: (UP + hop, DOWN + hop), 3: (DOWN + hop, e_slot)}
        q_order = {1: (e_q, q), 2: (q, q), 3: (q, e_q)}
        return (
            jnp.where(last, order[position][1], order[position][0]),
            jnp.where(last, q_order[position][1], q_order[position][0]),
        )

    def ready(k, position):
        slot, q = place(k, position)
        if position == 0:
            @pl.when(k > 0)
            def _():
                relay(k)

            arrived(slot, q)
        elif position == 1:
            @pl.when(k < passes - 1)
            def _():
                arrived(slot, q)
        elif position == 2:
            @pl.when(k == 0)
            def _():
                relay(k)
        else:
            @pl.when(k == passes - 1)
            def _():
                arrived(slot, q)

    def prep(k, position):
        slot, q = place(k, position)
        prepare(buf[slot, q], scale_ref, rhs_d[position % 2], rhs_c[position % 2], vis[position])

    inverse = 1.0 / column_of(length[...], dim)
    scale_ref[...] = jnp.broadcast_to(inverse * UNIT, (dim, CHUNK))
    own_side(buf, scale_ref, lhs_d, lhs_c, chunks, probe_count)
    total[...] = jnp.zeros_like(total)
    w1[...] = jnp.zeros_like(w1)
    sub = lax.broadcasted_iota(jnp.int32, (16, 2 * CHUNK), 0)
    for v in vis:
        v[64:80, :] = jnp.where(sub == 0, 1.0, 0.0).astype(BF16)
    v3[0:64, :] = jnp.zeros((64, 2 * CHUNK), BF16)

    ready(0, 0)
    prep(0, 0)
    products(lhs_d, lhs_c, rhs_d0, rhs_c0, dist0, coup0)
    ready(0, 1)
    prep(0, 1)

    @pl.loop(0, passes)
    def _(k):
        for position in range(4):
            here, there = position % 2, (position + 1) % 2
            ahead = (position + 2) % 4
            if position < 2:
                k_ahead = k
                ready(k, ahead)
            else:
                k_ahead = jnp.minimum(k + 1, passes - 1)

                @pl.when(k < passes - 1)
                def _():
                    ready(k + 1, ahead)

            gather_sums(vis[(position + 3) % 4], w[there], total)
            products(lhs_d, lhs_c, rhs_d[there], rhs_c[there], dist[there], coup[there])
            weigh(dist[here], coup[here], w[here])
            prep(k_ahead, ahead)

    gather_sums(v3, w1, total)

    for q in range(chunks):
        lanes = slice(q * CHUNK, (q + 1) * CHUNK)
        scaled = buf[OWN, q, 0:32, :] * scale_ref[...]
        summed = scaled * total[64:65, lanes] - (total[0:32, lanes] + total[32:64, lanes])
        out[:, lanes] = scale_ref[...] * (-5.0 / (3.0 * UNIT * UNIT)) * summed

    for q in range(chunks):
        send(OWN, PARTNER, q, partner).wait_send()
        for hop in range(hops):
            send(OWN, UP + hop, q, above).wait_send()
            send(OWN, DOWN + hop, q, below).wait_send()
            if hop < hops - 1:
                send(OWN, P_UP + hop, q, partner).wait_send()
                send(OWN, P_DOWN + hop, q, partner).wait_send()
        send(give_src, give_dst, q, partner).wait_send()


def scratch_shapes(dim, points):
    chunks = points // CHUNK
    return [
        pltpu.VMEM((SLOTS, chunks, 64, CHUNK), F32),
        pltpu.VMEM((dim, CHUNK), F32),
        pltpu.VMEM((points, 256), BF16),
        pltpu.VMEM((points, 128), BF16),
        *[pltpu.VMEM((DEPTH, CHUNK), BF16)] * 2,
        *[pltpu.VMEM((128, CHUNK), BF16)] * 2,
        *[pltpu.VMEM((80, 2 * CHUNK), BF16)] * 4,
        *[pltpu.VMEM((points, CHUNK), F32)] * 4,
        *[pltpu.VMEM((points, 2 * CHUNK), BF16)] * 2,
        pltpu.VMEM((80, points), F32),
        pltpu.SemaphoreType.DMA((SLOTS, chunks)),
        pltpu.SemaphoreType.DMA((SLOTS, chunks)),
    ]


def on_device(coords, alpha, probe_solves, probes, lengthscale):
    dim, points = coords.shape
    vmem_spec = pl.BlockSpec(memory_space=pltpu.VMEM)
    return pl.pallas_call(
        functools.partial(kernel, lax.axis_size("blk")),
        out_shape=jax.ShapeDtypeStruct((dim, points), F32),
        in_specs=[vmem_spec] * 5,
        out_specs=vmem_spec,
        scratch_shapes=scratch_shapes(dim, points),
        compiler_params=pltpu.CompilerParams(collective_id=0, has_side_effects=True),
    )(coords, alpha[None], probe_solves, probes, lengthscale[None])


def solution(mesh):
    return jax.shard_map(
        on_device,
        mesh=mesh,
        in_specs=(
            P(None, ("groups", "blk")),
            P(("groups", "blk")),
            P(None, ("groups", "blk")),
            P(None, ("groups", "blk")),
            P(),
        ),
        out_specs=P(None, ("groups", "blk")),
        check_vma=False,
    )
```

time: 130 us -> 63.7 us (0.49)
  matrix products: 74.4 us -> 0 us
  Pallas kernels: 0 us -> 60.3 us
  starting transfers between devices: 30.7 us -> 0 us
  waiting for transfers between devices: 17.8 us -> 0 us
  other arithmetic: 4.33 us -> 0 us
  local copies, waits for them, and re-layouts: 0.9 us -> 2.81 us
    dot_general x32 -> x0, matrix products: 74.4 us -> none  [the longest x8 28.1 us: tile_terms(): lax.dot_general(own_scaled, vis_scaled, contract_first, precision=lax.Pre...]
    pallas_call x0 -> x1, Pallas kernels: none -> 60.3 us  [on_device(): pl.pallas_call(functools.partial(kernel, lax.axis_size('blk')), out_shape...]
    ppermute x24 -> x0, starting transfers between devices: 30.7 us -> none  [shifted(): return lax.ppermute(value, axis, pairs)]
    ppermute x24 -> x0, waiting for transfers between devices: 17.8 us -> none  [shifted(): return lax.ppermute(value, axis, pairs)]
    mul x9 -> x0, other arithmetic: 1.66 us -> none  [the longest x8 0.95 us: tile_terms(): left_rows = jnp.concatenate([own_table[:1], -half_inv * own_table[1:]], 0)]
    unnamed x0 -> x1, local copies, waits for them, and re-layouts: none -> 1.54 us
  transfers between devices with their start and end apart: 24 -> 0, of which waited for: 8 -> 0; matrix products, arithmetic and copies ran while one was open for 55% -> 0% of each run, Pallas kernels for 0% -> 0%
where the time goes in v1:
time: 63.7 us; the launch traced here: 63.2 us
  Pallas kernels  60.3 us (95%)
  local copies, waits for them, and re-layouts  2.81 us (4%)
    pallas_call x1, Pallas kernels, on_device(): pl.pallas_call(functools.partial(kernel, lax.axis_size('blk')), out_shape...  60.3 us
    unnamed x1, local copies, waits for them, and re-layouts  1.54 us

profile of v1, /device:TPU:69, one launch (start us, length us, event | category | flops | bytes accessed | tf_op | source)
XLA Modules:
  0.0 63.2 jit_solution(11843658132775366172)
XLA Ops:
  0.0 1.3 %broadcast_in_dim.6.alpha = f32[1,768]{1,0:T(1,128)} reshape(f32[768]{0:T(1024)} %param.6) | data formatting | bytes 6144 | tf_op jit(solution)/shard_map/broadcast_in_dim | solution.py:317
  1.3 60.3 %shard_map.55 = f32[32,768]{1,0:T(8,128)} custom-call(f32[32,768]{1,0:T(8,128)} %coords.1, f32[1,768]{1,0:T(1,128)} %broadcast_in_dim.6.alpha, f32[15,768]{1,0:T(8,128)} %solves.1, f32[15,768]{1,0:T(8,128)} %probes.1, f32[1,32]{1,0:T(1,128)} %bitcast.1), custom_call_target="tpu_custom_call" | custom-call | tf_op jit(solution)/shard_map/pallas_call | solution.py:310
  61.6 1.5 %copy.7 = f32[32,768]{1,0:T(8,128)} copy(f32[32,768]{1,0:T(8,128)} %shard_map.55) | data formatting | bytes 196608

commit v2 on v1

--- a/solution.py
+++ b/solution.py
@@ -48,54 +48,61 @@
     return out
 
 
-def prepare(block, scale_ref, rhs_d, rhs_c, vis):
+def prepare(block, scale_ref, lhs_d, lhs_c, vis):
     scaled = block[0:32, :] * scale_ref[...]
     hi, mid, lo = split3(scaled)
-    for index, value in enumerate((hi, mid, lo, hi, mid, hi)):
-        rhs_d[32 * index : 32 * index + 32, :] = value
-    n_hi, n_mid, n_lo = split3(jnp.sum(scaled * scaled, 0, keepdims=True))
-    ends = (1.0, 1.0, 1.0, n_hi.astype(F32), n_mid.astype(F32), n_lo.astype(F32))
-    rhs_d[192:208, :] = pick_rows(ends, (16, CHUNK)).astype(BF16)
+    norm = [v.astype(F32) for v in split3(jnp.sum(scaled * scaled, 0, keepdims=True))]
+    ends = pick_rows((1.0, 1.0, 1.0, *norm), (64, CHUNK)).astype(BF16)
+    lhs_d[...] = jnp.concatenate([hi, mid, lo, hi, mid, hi, ends], 0).T
     t_hi, t_lo = split2(block[32:64, :])
-    for index, value in enumerate((t_hi, t_lo, t_hi, t_lo)):
-        rhs_c[32 * index : 32 * index + 32, :] = value
+    lhs_c[...] = jnp.concatenate([t_hi, t_lo, t_hi, t_lo], 0).T
     for side in (0, CHUNK):
         vis[0:32, side : side + CHUNK] = hi
         vis[32:64, side : side + CHUNK] = mid
 
 
-def products(lhs_d, lhs_c, rhs_d, rhs_c, dist, coup):
-    dist[...] = jnp.dot(lhs_d[:, 0:DEPTH], rhs_d[...], preferred_element_type=F32)
-    coup[...] = jnp.dot(lhs_c[...], rhs_c[...], preferred_element_type=F32)
-
-
-def weigh(dist, coup, w, rows=128):
-    for start in range(0, dist.shape[0], rows):
-        part = pl.ds(start, rows)
-        d2 = jnp.maximum(dist[part, :], 1e-30)
-        u = d2 * lax.rsqrt(d2)
-        weight = (1.0 / LN2 + u) * jnp.exp2(-u) * coup[part, :]
-        hi, lo = split2(weight)
-        w[part, 0:CHUNK] = hi
-        w[part, CHUNK : 2 * CHUNK] = lo
-
-
-def gather_sums(vis, w, total):
-    total[...] += lax.dot_general(
-        vis[...], w[...], (((1,), (1,)), ((), ())), preferred_element_type=F32
-    )
-
-
-def own_side(buf, scale_ref, lhs_d, lhs_c, chunks, probe_count):
+def products(lhs_d, lhs_c, rhs_d, rhs_c, dist, coup, lanes):
+    dist[:, lanes] = jnp.dot(lhs_d[:, 0:DEPTH], rhs_d[:, lanes], preferred_element_type=F32)
+    coup[:, lanes] = jnp.dot(lhs_c[...], rhs_c[:, lanes], preferred_element_type=F32)
+
+
+def weigh(dist, coup, w, rows, lanes):
+    d2 = jnp.maximum(dist[rows, lanes], 1e-30)
+    u = d2 * lax.rsqrt(d2)
+    weight = (1.0 / LN2 + u) * jnp.exp2(-u) * coup[rows, lanes]
+    hi, lo = split2(weight)
+    w[rows, lanes] = hi
+    w[rows.start + CHUNK : rows.stop + CHUNK, lanes] = lo
+
+
+def gather_sums(vis, w, total, lanes):
+    total[:, lanes] += jnp.dot(vis[...], w[:, lanes], preferred_element_type=F32)
+
+
+def region(vis, w_old, total, lhs_d, lhs_c, rhs_d, rhs_c, dist, coup, dist_old, coup_old, w, prep):
+    def dots(r, n=256):
+        products(lhs_d, lhs_c, rhs_d, rhs_c, dist, coup, slice(r, r + n))
+    def gat(r, n=256):
+        gather_sums(vis, w_old, total, slice(r, r + n))
+    def wei(l, n=256, r=0, m=256, step=32):
+        for t in range(r, r + m, step):
+            weigh(dist_old, coup_old, w, slice(t, t + step), slice(l, l + n))
+    for t in range(0, 768, 256):
+        dots(t)
+        gat(t)
+        wei(t)
+    prep()
+
+def own_side(buf, scale_ref, rhs_d, rhs_c, chunks, probe_count):
     sub = lax.broadcasted_iota(jnp.int32, (32, CHUNK), 0)
     for q in range(chunks):
+        lanes = slice(q * CHUNK, (q + 1) * CHUNK)
         block = buf[OWN, q]
         scaled = block[0:32, :] * scale_ref[...]
-        hi, mid, lo = (-2.0 * v.astype(F32) for v in split3(scaled))
+        hi, mid, lo = ((-2.0 * v.astype(F32)).astype(BF16) for v in split3(scaled))
         norm = [v.astype(F32) for v in split3(jnp.sum(scaled * scaled, 0, keepdims=True))]
-        ends = pick_rows((*norm, 1.0, 1.0, 1.0), (64, CHUNK))
-        stack = jnp.concatenate([hi, hi, hi, mid, mid, lo, ends], 0)
-        lhs_d[q * CHUNK : (q + 1) * CHUNK, :] = stack.T.astype(BF16)
+        ends = pick_rows((*norm, 1.0, 1.0, 1.0), (16, CHUNK)).astype(BF16)
+        rhs_d[:, lanes] = jnp.concatenate([hi, hi, hi, mid, mid, lo, ends], 0)
         swapped = jnp.concatenate([block[48:64, :], block[32:48, :]], 0)
         half_inv = LN2 / (2.0 * probe_count)
         table = jnp.where(
@@ -103,15 +110,14 @@
             LN2 * swapped,
             jnp.where(sub == 2 * probe_count + 1, 0.0, -half_inv * swapped),
         )
-        t_hi, t_lo = (v.astype(F32) for v in split2(table))
-        stack = jnp.concatenate([t_hi, t_hi, t_lo, t_lo], 0)
-        lhs_c[q * CHUNK : (q + 1) * CHUNK, :] = stack.T.astype(BF16)
+        t_hi, t_lo = split2(table)
+        rhs_c[:, lanes] = jnp.concatenate([t_hi, t_hi, t_lo, t_lo], 0)
 
 
 def kernel(size, coords, alpha, solves, probes, length, out, *scratch):
-    (buf, scale_ref, lhs_d, lhs_c, rhs_d0, rhs_d1, rhs_c0, rhs_c1, v0, v1, v2, v3,
+    (buf, scale_ref, rhs_d, rhs_c, lhs_d0, lhs_d1, lhs_c0, lhs_c1, v0, v1, v2, v3,
      dist0, dist1, coup0, coup1, w0, w1, total, send_sem, recv_sem) = scratch
-    rhs_d, rhs_c, vis = (rhs_d0, rhs_d1), (rhs_c0, rhs_c1), (v0, v1, v2, v3)
+    lhs_d, lhs_c, vis = (lhs_d0, lhs_d1), (lhs_c0, lhs_c1), (v0, v1, v2, v3)
     dist, coup, w = (dist0, dist1), (coup0, coup1), (w0, w1)
     dim, points = coords.shape
     probe_count = solves.shape[0]
@@ -128,9 +134,10 @@
 
     for q in range(chunks):
         lanes = slice(q * CHUNK, (q + 1) * CHUNK)
+        row = alpha[lanes].reshape(1, CHUNK)
         buf[OWN, q, 0:32, :] = coords[:, lanes]
         buf[OWN, q, 32:64, :] = jnp.concatenate(
-            [solves[:, lanes], alpha[:, lanes], probes[:, lanes], alpha[:, lanes]], 0
+            [solves[:, lanes], row, probes[:, lanes], row], 0
         )
 
     barrier = pltpu.get_barrier_semaphore()
@@ -229,11 +236,11 @@
 
     def prep(k, position):
         slot, q = place(k, position)
-        prepare(buf[slot, q], scale_ref, rhs_d[position % 2], rhs_c[position % 2], vis[position])
+        prepare(buf[slot, q], scale_ref, lhs_d[position % 2], lhs_c[position % 2], vis[position])
 
     inverse = 1.0 / column_of(length[...], dim)
     scale_ref[...] = jnp.broadcast_to(inverse * UNIT, (dim, CHUNK))
-    own_side(buf, scale_ref, lhs_d, lhs_c, chunks, probe_count)
+    own_side(buf, scale_ref, rhs_d, rhs_c, chunks, probe_count)
     total[...] = jnp.zeros_like(total)
     w1[...] = jnp.zeros_like(w1)
     sub = lax.broadcasted_iota(jnp.int32, (16, 2 * CHUNK), 0)
@@ -243,7 +250,7 @@
 
     ready(0, 0)
     prep(0, 0)
-    products(lhs_d, lhs_c, rhs_d0, rhs_c0, dist0, coup0)
+    products(lhs_d0, lhs_c0, rhs_d, rhs_c, dist0, coup0, slice(0, points))
     ready(0, 1)
     prep(0, 1)
 
@@ -252,22 +259,20 @@
         for position in range(4):
             here, there = position % 2, (position + 1) % 2
             ahead = (position + 2) % 4
-            if position < 2:
-                k_ahead = k
-                ready(k, ahead)
-            else:
-                k_ahead = jnp.minimum(k + 1, passes - 1)
-
+            if position == 0:
+                ready(k, 2)
+                ready(k, 3)
+            elif position == 2:
                 @pl.when(k < passes - 1)
                 def _():
-                    ready(k + 1, ahead)
-
-            gather_sums(vis[(position + 3) % 4], w[there], total)
-            products(lhs_d, lhs_c, rhs_d[there], rhs_c[there], dist[there], coup[there])
-            weigh(dist[here], coup[here], w[here])
-            prep(k_ahead, ahead)
-
-    gather_sums(v3, w1, total)
+                    ready(k + 1, 0)
+                    ready(k + 1, 1)
+            k_ahead = k if position < 2 else jnp.minimum(k + 1, passes - 1)
+            region(vis[(position + 3) % 4], w[there], total, lhs_d[there], lhs_c[there], rhs_d, rhs_c,
+                   dist[there], coup[there], dist[here], coup[here], w[here],
+                   lambda: prep(k_ahead, ahead))
+
+    gather_sums(v3, w1, total, slice(0, points))
 
     for q in range(chunks):
         lanes = slice(q * CHUNK, (q + 1) * CHUNK)
@@ -291,13 +296,13 @@
     return [
         pltpu.VMEM((SLOTS, chunks, 64, CHUNK), F32),
         pltpu.VMEM((dim, CHUNK), F32),
-        pltpu.VMEM((points, 256), BF16),
-        pltpu.VMEM((points, 128), BF16),
-        *[pltpu.VMEM((DEPTH, CHUNK), BF16)] * 2,
-        *[pltpu.VMEM((128, CHUNK), BF16)] * 2,
+        pltpu.VMEM((DEPTH, points), BF16),
+        pltpu.VMEM((128, points), BF16),
+        *[pltpu.VMEM((CHUNK, 256), BF16)] * 2,
+        *[pltpu.VMEM((CHUNK, 128), BF16)] * 2,
         *[pltpu.VMEM((80, 2 * CHUNK), BF16)] * 4,
-        *[pltpu.VMEM((points, CHUNK), F32)] * 4,
-        *[pltpu.VMEM((points, 2 * CHUNK), BF16)] * 2,
+        *[pltpu.VMEM((CHUNK, points), F32)] * 4,
+        *[pltpu.VMEM((2 * CHUNK, points), BF16)] * 2,
         pltpu.VMEM((80, points), F32),
         pltpu.SemaphoreType.DMA((SLOTS, chunks)),
         pltpu.SemaphoreType.DMA((SLOTS, chunks)),
@@ -314,7 +319,7 @@
         out_specs=vmem_spec,
         scratch_shapes=scratch_shapes(dim, points),
         compiler_params=pltpu.CompilerParams(collective_id=0, has_side_effects=True),
-    )(coords, alpha[None], probe_solves, probes, lengthscale[None])
+    )(coords, alpha, probe_solves, probes, lengthscale[None])
 
 
 def solution(mesh):

time: 63.7 us -> 49.1 us (0.77)
  Pallas kernels: 60.3 us -> 47.4 us
  local copies, waits for them, and re-layouts: 2.81 us -> 1.54 us
    pallas_call x1, Pallas kernels: 60.3 us -> 47.4 us  [on_device(): pl.pallas_call(functools.partial(kernel, lax.axis_size('blk')), out_shape...]
    broadcast_in_dim x1 -> x0, local copies, waits for them, and re-layouts: 1.27 us -> none  [on_device(): alpha[None]]
where the time goes in v2:
time: 49.1 us; the launch traced here: 48.9 us
  Pallas kernels  47.4 us (97%)
  local copies, waits for them, and re-layouts  1.54 us (3%)
    pallas_call x1, Pallas kernels, on_device(): pl.pallas_call(functools.partial(kernel, lax.axis_size('blk')), out_shape...  47.4 us
    unnamed x1, local copies, waits for them, and re-layouts  1.54 us

profile of v2, /device:TPU:69, one launch (start us, length us, event | category | flops | bytes accessed | tf_op | source)
XLA Modules:
  0.0 48.9 jit_solution(8121900192863132522)
XLA Ops:
  0.0 47.4 %shard_map.55 = f32[32,768]{1,0:T(8,128)} custom-call(f32[32,768]{1,0:T(8,128)} %coords.1, f32[768]{0:T(1024)} %alpha.1, f32[15,768]{1,0:T(8,128)} %solves.1, f32[15,768]{1,0:T(8,128)} %probes.1, f32[1,32]{1,0:T(1,128)} %bitcast.1), custom_call_target="tpu_custom_call" | custom-call | tf_op jit(solution)/shard_map/pallas_call | solution.py:315
  47.4 1.5 %copy.7 = f32[32,768]{1,0:T(8,128)} copy(f32[32,768]{1,0:T(8,128)} %shard_map.55) | data formatting | bytes 196608

commit v3 on v2

--- a/solution.py
+++ b/solution.py
@@ -52,8 +52,10 @@
     scaled = block[0:32, :] * scale_ref[...]
     hi, mid, lo = split3(scaled)
     norm = [v.astype(F32) for v in split3(jnp.sum(scaled * scaled, 0, keepdims=True))]
-    ends = pick_rows((1.0, 1.0, 1.0, *norm), (64, CHUNK)).astype(BF16)
-    lhs_d[...] = jnp.concatenate([hi, mid, lo, hi, mid, hi, ends], 0).T
+    ends = pick_rows((1.0, 1.0, 1.0, *norm), (8, CHUNK))
+    ends = jnp.concatenate([ends, jnp.zeros((8, CHUNK), F32)], 0).astype(BF16)
+    rest = jnp.zeros((256 - DEPTH, CHUNK), BF16)
+    lhs_d[...] = jnp.concatenate([hi, mid, lo, hi, mid, hi, ends, rest], 0).T
     t_hi, t_lo = split2(block[32:64, :])
     lhs_c[...] = jnp.concatenate([t_hi, t_lo, t_hi, t_lo], 0).T
     for side in (0, CHUNK):
@@ -62,12 +64,13 @@
 
 
 def products(lhs_d, lhs_c, rhs_d, rhs_c, dist, coup, lanes):
-    dist[:, lanes] = jnp.dot(lhs_d[:, 0:DEPTH], rhs_d[:, lanes], preferred_element_type=F32)
+    d2 = jnp.dot(lhs_d[:, 0:DEPTH], rhs_d[:, lanes], preferred_element_type=F32)
+    dist[:, lanes] = jnp.maximum(d2, 1e-30)
     coup[:, lanes] = jnp.dot(lhs_c[...], rhs_c[:, lanes], preferred_element_type=F32)
 
 
 def weigh(dist, coup, w, rows, lanes):
-    d2 = jnp.maximum(dist[rows, lanes], 1e-30)
+    d2 = dist[rows, lanes]
     u = d2 * lax.rsqrt(d2)
     weight = (1.0 / LN2 + u) * jnp.exp2(-u) * coup[rows, lanes]
     hi, lo = split2(weight)
@@ -79,7 +82,7 @@
     total[:, lanes] += jnp.dot(vis[...], w[:, lanes], preferred_element_type=F32)
 
 
-def region(vis, w_old, total, lhs_d, lhs_c, rhs_d, rhs_c, dist, coup, dist_old, coup_old, w, prep):
+def region(vis, w_old, total, lhs_d, lhs_c, rhs_d, rhs_c, dist, coup, dist_old, coup_old, w, prep, products_ahead):
     def dots(r, n=256):
         products(lhs_d, lhs_c, rhs_d, rhs_c, dist, coup, slice(r, r + n))
     def gat(r, n=256):
@@ -87,11 +90,14 @@
     def wei(l, n=256, r=0, m=256, step=32):
         for t in range(r, r + m, step):
             weigh(dist_old, coup_old, w, slice(t, t + step), slice(l, l + n))
-    for t in range(0, 768, 256):
-        dots(t)
+    for t in range(0, w.shape[1], CHUNK):
+        if products_ahead:
+            dots(t)
         gat(t)
         wei(t)
-    prep()
+    if prep is not None:
+        prep()
+
 
 def own_side(buf, scale_ref, rhs_d, rhs_c, chunks, probe_count):
     sub = lax.broadcasted_iota(jnp.int32, (32, CHUNK), 0)
@@ -114,9 +120,10 @@
         rhs_c[:, lanes] = jnp.concatenate([t_hi, t_hi, t_lo, t_lo], 0)
 
 
-def kernel(size, coords, alpha, solves, probes, length, out, *scratch):
+def kernel(size, coords_in, alpha_in, solves_in, probes_in, length_in, out, *scratch):
     (buf, scale_ref, rhs_d, rhs_c, lhs_d0, lhs_d1, lhs_c0, lhs_c1, v0, v1, v2, v3,
-     dist0, dist1, coup0, coup1, w0, w1, total, send_sem, recv_sem) = scratch
+     dist0, dist1, coup0, coup1, w0, w1, total, coords, alpha, solves, probes, length,
+     in_sem, send_sem, recv_sem) = scratch
     lhs_d, lhs_c, vis = (lhs_d0, lhs_d1), (lhs_c0, lhs_c1), (v0, v1, v2, v3)
     dist, coup, w = (dist0, dist1), (coup0, coup1), (w0, w1)
     dim, points = coords.shape
@@ -132,6 +139,22 @@
     below = lax.rem(me + size - 2, size)
     partner = me + 1 - 2 * core
 
+    barrier = pltpu.get_barrier_semaphore()
+    for other in (above, below, partner):
+        pl.semaphore_signal(barrier, inc=1, device_id=(group, other), device_id_type=MESH)
+
+    loads = [
+        pltpu.make_async_copy(src, dst, in_sem.at[index])
+        for index, (src, dst) in enumerate(
+            ((coords_in, coords), (alpha_in, alpha), (solves_in, solves), (probes_in, probes),
+             (length_in, length))
+        )
+    ]
+    for load in loads:
+        load.start()
+    for load in loads:
+        load.wait()
+
     for q in range(chunks):
         lanes = slice(q * CHUNK, (q + 1) * CHUNK)
         row = alpha[lanes].reshape(1, CHUNK)
@@ -140,9 +163,6 @@
             [solves[:, lanes], row, probes[:, lanes], row], 0
         )
 
-    barrier = pltpu.get_barrier_semaphore()
-    for other in (above, below, partner):
-        pl.semaphore_signal(barrier, inc=1, device_id=(group, other), device_id_type=MESH)
     pl.semaphore_wait(barrier, 3)
 
     def send(src, dst, q, other):
@@ -167,76 +187,36 @@
     give_dst = jnp.where(core == 0, P_DOWN + hops - 1, P_UP + hops - 1)
     take = jnp.where(core == 0, P_UP + hops - 1, P_DOWN + hops - 1)
 
-    def relay(k):
+    def relay(k, last_hop):
         hop, q = k // chunks, lax.rem(k, chunks)
         arrived(UP + hop, q)
-
-        @pl.when(hop < hops - 1)
-        def _():
+        if not last_hop:
             send(UP + hop, UP + hop + 1, q, above).start()
-
         arrived(DOWN + hop, q)
-
-        @pl.when(hop < hops - 1)
-        def _():
+        if last_hop:
+            send(give_src, give_dst, q, partner).start()
+        else:
             send(DOWN + hop, DOWN + hop + 1, q, below).start()
             send(UP + hop, P_UP + hop, q, partner).start()
             send(DOWN + hop, P_DOWN + hop, q, partner).start()
 
-        @pl.when(hop == hops - 1)
-        def _():
-            send(give_src, give_dst, q, partner).start()
-
-    def extra(e):
-        pair = jnp.maximum(e - chunks, 0)
-        k = pair // 2
-        lane = jnp.where(lax.rem(pair, 2) == 0, P_UP, P_DOWN)
-        tail = e - chunks - 2 * (passes - chunks)
-        slot = jnp.where(
-            e < chunks,
-            PARTNER,
-            jnp.where(tail < 0, lane + k // chunks, take),
-        )
-        q = jnp.where(e < chunks, e, jnp.where(tail < 0, lax.rem(k, chunks), tail))
-        return slot, q
-
-    def place(k, position):
-        e_slot, e_q = extra(2 * k + (1 if position else 0))
-        hop, q = k // chunks, lax.rem(k, chunks)
-        if position == 0:
-            return e_slot, e_q
-        last = k == passes - 1
-        order = {1: (e_slot, UP + hop), 2: (UP + hop, DOWN + hop), 3: (DOWN + hop, e_slot)}
-        q_order = {1: (e_q, q), 2: (q, q), 3: (q, e_q)}
-        return (
-            jnp.where(last, order[position][1], order[position][0]),
-            jnp.where(last, q_order[position][1], q_order[position][0]),
-        )
-
-    def ready(k, position):
-        slot, q = place(k, position)
-        if position == 0:
-            @pl.when(k > 0)
-            def _():
-                relay(k)
-
-            arrived(slot, q)
-        elif position == 1:
-            @pl.when(k < passes - 1)
-            def _():
-                arrived(slot, q)
-        elif position == 2:
-            @pl.when(k == 0)
-            def _():
-                relay(k)
-        else:
-            @pl.when(k == passes - 1)
-            def _():
-                arrived(slot, q)
-
-    def prep(k, position):
-        slot, q = place(k, position)
+    def prep(slot, q, position):
         prepare(buf[slot, q], scale_ref, lhs_d[position % 2], lhs_c[position % 2], vis[position])
+
+    def step(position, slot=None, q=None, more=True):
+        here, there = position % 2, (position + 1) % 2
+        ahead = None if slot is None else lambda: prep(slot, q, (position + 2) % 4)
+        region(vis[(position + 3) % 4], w[there], total, lhs_d[there], lhs_c[there], rhs_d, rhs_c,
+               dist[there], coup[there], dist[here], coup[here], w[here], ahead, more)
+
+    def up(k):
+        return UP + k // chunks, lax.rem(k, chunks)
+
+    def down(k):
+        return DOWN + k // chunks, lax.rem(k, chunks)
+
+    def side(k):
+        return (P_UP + k // chunks, lax.rem(k, chunks)), (P_DOWN + k // chunks, lax.rem(k, chunks))
 
     inverse = 1.0 / column_of(length[...], dim)
     scale_ref[...] = jnp.broadcast_to(inverse * UNIT, (dim, CHUNK))
@@ -248,30 +228,48 @@
         v[64:80, :] = jnp.where(sub == 0, 1.0, 0.0).astype(BF16)
     v3[0:64, :] = jnp.zeros((64, 2 * CHUNK), BF16)
 
-    ready(0, 0)
-    prep(0, 0)
+    for q in range(chunks):
+        arrived(PARTNER, q)
+    prep(PARTNER, 0, 0)
     products(lhs_d0, lhs_c0, rhs_d, rhs_c, dist0, coup0, slice(0, points))
-    ready(0, 1)
-    prep(0, 1)
-
-    @pl.loop(0, passes)
+    prep(PARTNER, 1, 1)
+    step(0, PARTNER, 2)
+    relay(0, False)
+    step(1, UP, 0)
+    step(2, DOWN, 0)
+    relay(1, False)
+    step(3, UP, 1)
+    step(0, DOWN, 1)
+
+    def turn(k, last_hop):
+        left, right = side(k - 1)
+        arrived(*left)
+        arrived(*right)
+        step(1, *left)
+        step(2, *right)
+        relay(k + 1, last_hop)
+        step(3, *up(k + 1))
+        step(0, *down(k + 1))
+
+    @pl.loop(1, passes - chunks - 1)
     def _(k):
-        for position in range(4):
-            here, there = position % 2, (position + 1) % 2
-            ahead = (position + 2) % 4
-            if position == 0:
-                ready(k, 2)
-                ready(k, 3)
-            elif position == 2:
-                @pl.when(k < passes - 1)
-                def _():
-                    ready(k + 1, 0)
-                    ready(k + 1, 1)
-            k_ahead = k if position < 2 else jnp.minimum(k + 1, passes - 1)
-            region(vis[(position + 3) % 4], w[there], total, lhs_d[there], lhs_c[there], rhs_d, rhs_c,
-                   dist[there], coup[there], dist[here], coup[here], w[here],
-                   lambda: prep(k_ahead, ahead))
-
+        turn(k, False)
+
+    @pl.loop(passes - chunks - 1, passes - chunks + 1)
+    def _(k):
+        turn(k, True)
+
+    arrived(take, 0)
+    arrived(take, 1)
+    step(1, take, 0)
+    step(2, take, 1)
+    relay(passes - 1, True)
+    step(3, *up(passes - 1))
+    step(0, *down(passes - 1))
+    arrived(take, 2)
+    step(1, take, 2)
+    step(2)
+    step(3, more=False)
     gather_sums(v3, w1, total, slice(0, points))
 
     for q in range(chunks):
@@ -291,7 +289,7 @@
         send(give_src, give_dst, q, partner).wait_send()
 
 
-def scratch_shapes(dim, points):
+def scratch_shapes(dim, points, probe_count):
     chunks = points // CHUNK
     return [
         pltpu.VMEM((SLOTS, chunks, 64, CHUNK), F32),
@@ -304,6 +302,12 @@
         *[pltpu.VMEM((CHUNK, points), F32)] * 4,
         *[pltpu.VMEM((2 * CHUNK, points), BF16)] * 2,
         pltpu.VMEM((80, points), F32),
+        pltpu.VMEM((dim, points), F32),
+        pltpu.VMEM((points,), F32),
+        pltpu.VMEM((probe_count, points), F32),
+        pltpu.VMEM((probe_count, points), F32),
+        pltpu.VMEM((1, dim), F32),
+        pltpu.SemaphoreType.DMA((5,)),
         pltpu.SemaphoreType.DMA((SLOTS, chunks)),
         pltpu.SemaphoreType.DMA((SLOTS, chunks)),
     ]
@@ -311,13 +315,14 @@
 
 def on_device(coords, alpha, probe_solves, probes, lengthscale):
     dim, points = coords.shape
+    any_spec = pl.BlockSpec(memory_space=pl.ANY)
     vmem_spec = pl.BlockSpec(memory_space=pltpu.VMEM)
     return pl.pallas_call(
         functools.partial(kernel, lax.axis_size("blk")),
         out_shape=jax.ShapeDtypeStruct((dim, points), F32),
-        in_specs=[vmem_spec] * 5,
+        in_specs=[any_spec] * 5,
         out_specs=vmem_spec,
-        scratch_shapes=scratch_shapes(dim, points),
+        scratch_shapes=scratch_shapes(dim, points, probe_solves.shape[0]),
         compiler_params=pltpu.CompilerParams(collective_id=0, has_side_effects=True),
     )(coords, alpha, probe_solves, probes, lengthscale[None])
 

time: 49.1 us -> 46.5 us (0.947)
  Pallas kernels: 47.4 us -> 44.8 us
    pallas_call x1, Pallas kernels: 47.4 us -> 44.8 us  [on_device(): pl.pallas_call(functools.partial(kernel, lax.axis_size('blk')), out_shape...]
where the time goes in v3:
time: 46.5 us; the launch traced here: 46.3 us
  Pallas kernels  44.8 us (96%)
  local copies, waits for them, and re-layouts  1.54 us (3%)
    pallas_call x1, Pallas kernels, on_device(): pl.pallas_call(functools.partial(kernel, lax.axis_size('blk')), out_shape...  44.8 us
    unnamed x1, local copies, waits for them, and re-layouts  1.54 us

profile of v3, /device:TPU:69, one launch (start us, length us, event | category | flops | bytes accessed | tf_op | source)
XLA Modules:
  0.0 46.3 jit_solution(10216747437699709156)
XLA Ops:
  0.0 44.8 %shard_map.55 = f32[32,768]{1,0:T(8,128)} custom-call(f32[32,768]{1,0:T(8,128)} %coords_in.1, f32[768]{0:T(1024)} %alpha_in.1, f32[15,768]{1,0:T(8,128)} %solves_in.1, f32[15,768]{1,0:T(8,128)} %probes_in.1, f32[1,32]{1,0:T(1,128)} %bitcast.1), custom_call_target="tpu_custom_call" | custom-call | tf_op jit(solution)/shard_map/pallas_call | solution.py:320
  44.8 1.5 %copy.7 = f32[32,768]{1,0:T(8,128)} copy(f32[32,768]{1,0:T(8,128)} %shard_map.55) | data formatting | bytes 196608

commit v4 on v3

--- a/solution.py
+++ b/solution.py
@@ -63,40 +63,31 @@
         vis[32:64, side : side + CHUNK] = mid
 
 
-def products(lhs_d, lhs_c, rhs_d, rhs_c, dist, coup, lanes):
-    d2 = jnp.dot(lhs_d[:, 0:DEPTH], rhs_d[:, lanes], preferred_element_type=F32)
-    dist[:, lanes] = jnp.maximum(d2, 1e-30)
-    coup[:, lanes] = jnp.dot(lhs_c[...], rhs_c[:, lanes], preferred_element_type=F32)
-
-
-def weigh(dist, coup, w, rows, lanes):
-    d2 = dist[rows, lanes]
-    u = d2 * lax.rsqrt(d2)
-    weight = (1.0 / LN2 + u) * jnp.exp2(-u) * coup[rows, lanes]
-    hi, lo = split2(weight)
-    w[rows, lanes] = hi
-    w[rows.start + CHUNK : rows.stop + CHUNK, lanes] = lo
+def direct(lhs_d, lhs_c, rhs_d, rhs_c, w, lanes, floor_ref):
+    floor = jnp.concatenate([jnp.concatenate([floor_ref[...]] * (CHUNK // 128), 1)] * 4, 0)
+    dist = jnp.dot(lhs_d[:, 0:DEPTH], rhs_d[:, lanes], preferred_element_type=F32)
+    coup = jnp.dot(lhs_c[...], rhs_c[:, lanes], preferred_element_type=F32)
+    for start in range(0, CHUNK, 32):
+        rows = slice(start, start + 32)
+        d2 = jnp.maximum(dist[rows], floor)
+        u = d2 * lax.rsqrt(d2)
+        weight = (1.0 / LN2 + u) * jnp.exp2(-u) * coup[rows]
+        w[rows, lanes] = weight.astype(BF16)
+        lo = weight - w[rows, lanes].astype(F32)
+        w[start + CHUNK : start + 32 + CHUNK, lanes] = lo.astype(BF16)
 
 
 def gather_sums(vis, w, total, lanes):
     total[:, lanes] += jnp.dot(vis[...], w[:, lanes], preferred_element_type=F32)
 
 
-def region(vis, w_old, total, lhs_d, lhs_c, rhs_d, rhs_c, dist, coup, dist_old, coup_old, w, prep, products_ahead):
-    def dots(r, n=256):
-        products(lhs_d, lhs_c, rhs_d, rhs_c, dist, coup, slice(r, r + n))
-    def gat(r, n=256):
-        gather_sums(vis, w_old, total, slice(r, r + n))
-    def wei(l, n=256, r=0, m=256, step=32):
-        for t in range(r, r + m, step):
-            weigh(dist_old, coup_old, w, slice(t, t + step), slice(l, l + n))
-    for t in range(0, w.shape[1], CHUNK):
-        if products_ahead:
-            dots(t)
-        gat(t)
-        wei(t)
+def region(lhs_d, lhs_c, rhs_d, rhs_c, vis, vis_old, w, w_old, total, floor_ref, prep):
     if prep is not None:
         prep()
+    for t in range(0, w.shape[1], CHUNK):
+        lanes = slice(t, t + CHUNK)
+        direct(lhs_d, lhs_c, rhs_d, rhs_c, w, lanes, floor_ref)
+        gather_sums(vis_old, w_old, total, lanes)
 
 
 def own_side(buf, scale_ref, rhs_d, rhs_c, chunks, probe_count):
@@ -121,11 +112,11 @@
 
 
 def kernel(size, coords_in, alpha_in, solves_in, probes_in, length_in, out, *scratch):
-    (buf, scale_ref, rhs_d, rhs_c, lhs_d0, lhs_d1, lhs_c0, lhs_c1, v0, v1, v2, v3,
-     dist0, dist1, coup0, coup1, w0, w1, total, coords, alpha, solves, probes, length,
-     in_sem, send_sem, recv_sem) = scratch
-    lhs_d, lhs_c, vis = (lhs_d0, lhs_d1), (lhs_c0, lhs_c1), (v0, v1, v2, v3)
-    dist, coup, w = (dist0, dist1), (coup0, coup1), (w0, w1)
+    (buf, scale_ref, rhs_d, rhs_c, ld0, ld1, ld2, ld3, lc0, lc1, lc2, lc3, v0, v1, v2, v3,
+     w0, w1, total, coords, alpha, solves, probes, length,
+     floor_ref, in_sem, send_sem, recv_sem) = scratch
+    lhs_d, lhs_c, vis = (ld0, ld1, ld2, ld3), (lc0, lc1, lc2, lc3), (v0, v1, v2, v3)
+    w = (w0, w1)
     dim, points = coords.shape
     probe_count = solves.shape[0]
     chunks = points // CHUNK
@@ -201,13 +192,13 @@
             send(DOWN + hop, P_DOWN + hop, q, partner).start()
 
     def prep(slot, q, position):
-        prepare(buf[slot, q], scale_ref, lhs_d[position % 2], lhs_c[position % 2], vis[position])
+        prepare(buf[slot, q], scale_ref, lhs_d[position], lhs_c[position], vis[position])
 
     def step(position, slot=None, q=None, more=True):
         here, there = position % 2, (position + 1) % 2
         ahead = None if slot is None else lambda: prep(slot, q, (position + 2) % 4)
-        region(vis[(position + 3) % 4], w[there], total, lhs_d[there], lhs_c[there], rhs_d, rhs_c,
-               dist[there], coup[there], dist[here], coup[here], w[here], ahead, more)
+        region(lhs_d[position], lhs_c[position], rhs_d, rhs_c, vis[position], vis[(position + 3) % 4],
+               w[here], w[there], total, floor_ref, ahead)
 
     def up(k):
         return UP + k // chunks, lax.rem(k, chunks)
@@ -222,6 +213,7 @@
     scale_ref[...] = jnp.broadcast_to(inverse * UNIT, (dim, CHUNK))
     own_side(buf, scale_ref, rhs_d, rhs_c, chunks, probe_count)
     total[...] = jnp.zeros_like(total)
+    floor_ref[...] = jnp.full_like(floor_ref, 1e-30)
     w1[...] = jnp.zeros_like(w1)
     sub = lax.broadcasted_iota(jnp.int32, (16, 2 * CHUNK), 0)
     for v in vis:
@@ -231,7 +223,6 @@
     for q in range(chunks):
         arrived(PARTNER, q)
     prep(PARTNER, 0, 0)
-    products(lhs_d0, lhs_c0, rhs_d, rhs_c, dist0, coup0, slice(0, points))
     prep(PARTNER, 1, 1)
     step(0, PARTNER, 2)
     relay(0, False)
@@ -296,10 +287,9 @@
         pltpu.VMEM((dim, CHUNK), F32),
         pltpu.VMEM((DEPTH, points), BF16),
         pltpu.VMEM((128, points), BF16),
-        *[pltpu.VMEM((CHUNK, 256), BF16)] * 2,
-        *[pltpu.VMEM((CHUNK, 128), BF16)] * 2,
+        *[pltpu.VMEM((CHUNK, 256), BF16)] * 4,
+        *[pltpu.VMEM((CHUNK, 128), BF16)] * 4,
         *[pltpu.VMEM((80, 2 * CHUNK), BF16)] * 4,
-        *[pltpu.VMEM((CHUNK, points), F32)] * 4,
         *[pltpu.VMEM((2 * CHUNK, points), BF16)] * 2,
         pltpu.VMEM((80, points), F32),
         pltpu.VMEM((dim, points), F32),
@@ -307,6 +297,7 @@
         pltpu.VMEM((probe_count, points), F32),
         pltpu.VMEM((probe_count, points), F32),
         pltpu.VMEM((1, dim), F32),
+        pltpu.VMEM((8, 128), F32),
         pltpu.SemaphoreType.DMA((5,)),
         pltpu.SemaphoreType.DMA((SLOTS, chunks)),
         pltpu.SemaphoreType.DMA((SLOTS, chunks)),

time: 46.5 us -> 43.7 us (0.940)
  Pallas kernels: 44.8 us -> 42 us
    pallas_call x1, Pallas kernels: 44.8 us -> 42 us  [on_device(): pl.pallas_call(functools.partial(kernel, lax.axis_size('blk')), out_shape...]
where the time goes in v4:
time: 43.7 us; the launch traced here: 43.6 us
  Pallas kernels  42 us (96%)
  local copies, waits for them, and re-layouts  1.54 us (4%)
    pallas_call x1, Pallas kernels, on_device(): pl.pallas_call(functools.partial(kernel, lax.axis_size('blk')), out_shape...  42 us
    unnamed x1, local copies, waits for them, and re-layouts  1.54 us

profile of v4, /device:TPU:69, one launch (start us, length us, event | category | flops | bytes accessed | tf_op | source)
XLA Modules:
  0.0 43.6 jit_solution(13226206912719369544)
XLA Ops:
  0.0 42.0 %shard_map.55 = f32[32,768]{1,0:T(8,128)} custom-call(f32[32,768]{1,0:T(8,128)} %coords_in.1, f32[768]{0:T(1024)} %alpha_in.1, f32[15,768]{1,0:T(8,128)} %solves_in.1, f32[15,768]{1,0:T(8,128)} %probes_in.1, f32[1,32]{1,0:T(1,128)} %bitcast.1), custom_call_target="tpu_custom_call" | custom-call | tf_op jit(solution)/shard_map/pallas_call | solution.py:311
  42.0 1.5 %copy.7 = f32[32,768]{1,0:T(8,128)} copy(f32[32,768]{1,0:T(8,128)} %shard_map.55) | data formatting | bytes 196608

commit v5 on v4

--- a/solution.py
+++ b/solution.py
@@ -111,10 +111,10 @@
         rhs_c[:, lanes] = jnp.concatenate([t_hi, t_hi, t_lo, t_lo], 0)
 
 
-def kernel(size, coords_in, alpha_in, solves_in, probes_in, length_in, out, *scratch):
+def kernel(size, coords_in, alpha_in, solves_in, probes_in, length_in, grad, *scratch):
     (buf, scale_ref, rhs_d, rhs_c, ld0, ld1, ld2, ld3, lc0, lc1, lc2, lc3, v0, v1, v2, v3,
      w0, w1, total, coords, alpha, solves, probes, length,
-     floor_ref, in_sem, send_sem, recv_sem) = scratch
+     floor_ref, out, in_sem, out_sem, send_sem, recv_sem) = scratch
     lhs_d, lhs_c, vis = (ld0, ld1, ld2, ld3), (lc0, lc1, lc2, lc3), (v0, v1, v2, v3)
     w = (w0, w1)
     dim, points = coords.shape
@@ -181,12 +181,11 @@
     def relay(k, last_hop):
         hop, q = k // chunks, lax.rem(k, chunks)
         arrived(UP + hop, q)
-        if not last_hop:
-            send(UP + hop, UP + hop + 1, q, above).start()
         arrived(DOWN + hop, q)
         if last_hop:
             send(give_src, give_dst, q, partner).start()
         else:
+            send(UP + hop, UP + hop + 1, q, above).start()
             send(DOWN + hop, DOWN + hop + 1, q, below).start()
             send(UP + hop, P_UP + hop, q, partner).start()
             send(DOWN + hop, P_DOWN + hop, q, partner).start()
@@ -194,7 +193,7 @@
     def prep(slot, q, position):
         prepare(buf[slot, q], scale_ref, lhs_d[position], lhs_c[position], vis[position])
 
-    def step(position, slot=None, q=None, more=True):
+    def step(position, slot=None, q=None):
         here, there = position % 2, (position + 1) % 2
         ahead = None if slot is None else lambda: prep(slot, q, (position + 2) % 4)
         region(lhs_d[position], lhs_c[position], rhs_d, rhs_c, vis[position], vis[(position + 3) % 4],
@@ -228,9 +227,11 @@
     relay(0, False)
     step(1, UP, 0)
     step(2, DOWN, 0)
+    step(3)
+    step(0)
     relay(1, False)
-    step(3, UP, 1)
-    step(0, DOWN, 1)
+    prep(UP, 1, 1)
+    prep(DOWN, 1, 2)
 
     def turn(k, last_hop):
         left, right = side(k - 1)
@@ -260,7 +261,7 @@
     arrived(take, 2)
     step(1, take, 2)
     step(2)
-    step(3, more=False)
+    step(3)
     gather_sums(v3, w1, total, slice(0, points))
 
     for q in range(chunks):
@@ -268,6 +269,9 @@
         scaled = buf[OWN, q, 0:32, :] * scale_ref[...]
         summed = scaled * total[64:65, lanes] - (total[0:32, lanes] + total[32:64, lanes])
         out[:, lanes] = scale_ref[...] * (-5.0 / (3.0 * UNIT * UNIT)) * summed
+
+    store = pltpu.make_async_copy(out, grad, out_sem)
+    store.start()
 
     for q in range(chunks):
         send(OWN, PARTNER, q, partner).wait_send()
@@ -278,6 +282,7 @@
                 send(OWN, P_UP + hop, q, partner).wait_send()
                 send(OWN, P_DOWN + hop, q, partner).wait_send()
         send(give_src, give_dst, q, partner).wait_send()
+    store.wait()
 
 
 def scratch_shapes(dim, points, probe_count):
@@ -298,7 +303,9 @@
         pltpu.VMEM((probe_count, points), F32),
         pltpu.VMEM((1, dim), F32),
         pltpu.VMEM((8, 128), F32),
+        pltpu.VMEM((dim, points), F32),
         pltpu.SemaphoreType.DMA((5,)),
+        pltpu.SemaphoreType.DMA,
         pltpu.SemaphoreType.DMA((SLOTS, chunks)),
         pltpu.SemaphoreType.DMA((SLOTS, chunks)),
     ]
@@ -307,12 +314,11 @@
 def on_device(coords, alpha, probe_solves, probes, lengthscale):
     dim, points = coords.shape
     any_spec = pl.BlockSpec(memory_space=pl.ANY)
-    vmem_spec = pl.BlockSpec(memory_space=pltpu.VMEM)
     return pl.pallas_call(
         functools.partial(kernel, lax.axis_size("blk")),
         out_shape=jax.ShapeDtypeStruct((dim, points), F32),
         in_specs=[any_spec] * 5,
-        out_specs=vmem_spec,
+        out_specs=any_spec,
         scratch_shapes=scratch_shapes(dim, points, probe_solves.shape[0]),
         compiler_params=pltpu.CompilerParams(collective_id=0, has_side_effects=True),
     )(coords, alpha, probe_solves, probes, lengthscale[None])

time: 43.7 us -> 43.4 us (level)
  no operation moved by 1% of the time
where the time goes in v5:
time: 43.4 us; the launch traced here: 43.2 us
  Pallas kernels  41.7 us (96%)
  local copies, waits for them, and re-layouts  1.54 us (4%)
    pallas_call x1, Pallas kernels, on_device(): pl.pallas_call(functools.partial(kernel, lax.axis_size('blk')), out_shape...  41.7 us
    unnamed x1, local copies, waits for them, and re-layouts  1.54 us

profile of v5, /device:TPU:69, one launch (start us, length us, event | category | flops | bytes accessed | tf_op | source)
XLA Modules:
  0.0 43.2 jit_solution(13023447678074722755)
XLA Ops:
  0.0 41.7 %shard_map.55 = f32[32,768]{1,0:T(8,128)} custom-call(f32[32,768]{1,0:T(8,128)} %coords_in.1, f32[768]{0:T(1024)} %alpha_in.1, f32[15,768]{1,0:T(8,128)} %solves_in.1, f32[15,768]{1,0:T(8,128)} %probes_in.1, f32[1,32]{1,0:T(1,128)} %bitcast.1), custom_call_target="tpu_custom_call" | custom-call | tf_op jit(solution)/shard_map/pallas_call | solution.py:317
  41.7 1.5 %copy.7 = f32[32,768]{1,0:T(8,128)} copy(f32[32,768]{1,0:T(8,128)} %shard_map.55) | data formatting | bytes 196608
